TPU v7x, 32 devices: a whole 2x2x4 slice. The times are simulated.
32 devices in a mesh: dp: 8 (over z, x), vocab: 4 (over y, core).
Axes of the slice: x: 2, y: 2, z: 4, core: 2. Of those that a mesh axis runs over, the one named last changes fastest.
Arguments:
- hidden_states: bfloat16 [1024, 3584], P('dp', 'vocab'), may hold values from -750 to 750, as said below
- head_weight: bfloat16 [152064, 3584], P(('dp', 'vocab')), may hold values from -0.09375 to 0.09375
- token_ids: int32 [1024], P('dp'), may hold values from 0 to 152063
- response_mask: int32 [1024], P('dp'), may hold values 0 or 1
- rollout_logprobs: float32 [1024], P('dp'), may hold values from -14 to -6
- advantages: float32 [1024], P('dp'), may hold values from -6 to 6
Outputs:
- logprobs: float32 [1024], P('dp')
- tis_weight: float32 [1024], P('dp')
- loss: float32 [], replicated
Inputs may be any that keep to these rules, and one draw needn't show every extreme that they name: `hidden_states`: hidden states; some rows may be far larger than others.
All inputs are finite; a program needn't handle non-finite values. No bound on the sum of `response_mask` on one device may be relied on, other than what follows from the above.
Results may differ from a plain program's by a relative error of at most 0.0003.
Values may be sent and summed in bfloat16 or wider, within the bound.
A program may use at most 128 MiB of HBM per device.

v0:
```python
import jax
import jax.numpy as jnp
from jax import lax
from jax.sharding import PartitionSpec as P


def shard_stats(logits, ids_block, columns):
    matched = columns[None, :] == ids_block[:, None]
    picked = jnp.sum(jnp.where(matched, logits, 0.0), axis=1)
    peak = jnp.max(logits, axis=1)
    total = jnp.sum(jnp.exp(logits - peak[:, None]), axis=1)
    return (peak, total, picked)


def token_terms(logp, rollout, advant, mask):
    weight = jnp.minimum(jnp.exp(logp - rollout), 2.0)
    counted = mask.astype(jnp.float32)
    loss_part = -jnp.sum(counted * weight * advant * logp)
    return (weight, loss_part, jnp.sum(counted))


def body(hidden_states, head_weight, token_ids, response_mask, rollout_logprobs, advantages):
    rows_local = token_ids.shape[0]
    vocab_local = head_weight.shape[0]
    offset = lax.axis_index(("dp", "vocab")) * vocab_local
    own_columns = lax.iota(jnp.int32, vocab_local) + offset
    dp_index = lax.axis_index("dp")
    own_start = dp_index * rows_local
    all_ids, all_mask = (
        lax.all_gather(token_ids, "dp", axis=0, tiled=True),
        lax.all_gather(response_mask, "dp", axis=0, tiled=True),
    )
    all_rollout, all_advant = (
        lax.all_gather(rollout_logprobs, "dp", axis=0, tiled=True),
        lax.all_gather(advantages, "dp", axis=0, tiled=True),
    )
    full_rows = lax.all_gather(hidden_states, "vocab", axis=1, tiled=True)
    logits = jnp.einsum(
        "rd,vd->rv",
        lax.all_gather(full_rows, "dp", axis=0, tiled=True),
        head_weight,
        preferred_element_type=jnp.float32,
    )
    peak, total, picked = shard_stats(logits, all_ids, own_columns)
    peak, total, picked = (peak, total, picked)
    top = lax.pmax(peak, ("dp", "vocab"))
    total_sum, picked_sum = lax.psum((total * jnp.exp(peak - top), picked), ("dp", "vocab"))
    logprob_all = picked_sum - (top + jnp.log(total_sum))
    own_logp = lax.dynamic_slice_in_dim(logprob_all, own_start, rows_local, 0)
    weight_all, loss_sum, count = token_terms(logprob_all, all_rollout, all_advant, all_mask)
    weight = lax.dynamic_slice_in_dim(weight_all, own_start, rows_local, 0)
    loss = loss_sum / jnp.maximum(count, 1.0)
    return (own_logp, weight, loss)


def solution(mesh):
    placed = (P("dp", "vocab"), P(("dp", "vocab"), None), P("dp"), P("dp"), P("dp"), P("dp"))
    return jax.shard_map(
        body, mesh=mesh, in_specs=placed, out_specs=(P("dp"), P("dp"), P()), check_vma=False
    )
```

profile of v0, /device:TPU:0, one launch (start us, length us, event | category | flops | bytes accessed | tf_op | source)
XLA Modules:
  0.0 274.0 jit_solution(17611963197525337187)
XLA Ops:
  7.2 0.0 all-gather.6.cloned.1.call-start
  7.2 12.5 %all_gather.19 = bf16[128,3584]{1,0:T(8,128)(2,1)} all-gather(bf16[128,896]{1,0:T(8,128)(2,1)} %param.6), channel_id=1, replica_groups=mesh['dp'=8,'vocab'=4] {'vocab'}, dimensions={1}, use_global_device_ids=true | all-gather | bytes 1146880 | tf_op jit(solution)/shard_map/all_gather | solution.py:37
  19.7 0.0 all-gather.6.cloned.1.call-update
  19.7 21.4 %all-gather.2 = s32[8,1,128]{2,1,0:T(1,128)S(1)} all-gather(s32[1,1,128]{2,1,0:T(1,128)} %bitcast.15), channel_id=1, replica_groups=mesh['dp'=8,'vocab'=4] {'dp'}, dimensions={0}, use_global_device_ids=true | all-gather | bytes 4608 | tf_op jit(solution)/shard_map/all_gather | solution.py:31
  41.2 0.6 convert_reduce_fusion
  42.4 17.1 %all-gather = s32[8,1,128]{2,1,0:T(1,128)S(1)} all-gather(s32[1,1,128]{2,1,0:T(1,128)} %bitcast.16), channel_id=1, replica_groups=mesh['dp'=8,'vocab'=4] {'dp'}, dimensions={0}, use_global_device_ids=true | all-gather | bytes 4608 | tf_op jit(solution)/shard_map/all_gather | solution.py:30
  59.5 18.8 %all-gather.1 = f32[8,1,128]{2,1,0:T(1,128)S(1)} all-gather(f32[1,1,128]{2,1,0:T(1,128)} %bitcast.17), channel_id=1, replica_groups=mesh['dp'=8,'vocab'=4] {'dp'}, dimensions={0}, use_global_device_ids=true | all-gather | bytes 4608 | tf_op jit(solution)/shard_map/all_gather | solution.py:34
  78.3 17.3 %all-gather.3 = f32[8,1,128]{2,1,0:T(1,128)S(1)} all-gather(f32[1,1,128]{2,1,0:T(1,128)} %bitcast.18), channel_id=1, replica_groups=mesh['dp'=8,'vocab'=4] {'dp'}, dimensions={0}, use_global_device_ids=true | all-gather | bytes 4608 | tf_op jit(solution)/shard_map/all_gather | solution.py:35
  95.6 36.2 %all-gather.6.cloned.1.call-done = bf16[1024,3584]{1,0:T(8,128)(2,1)} async-done(((bf16[128,3584]{1,0:T(8,128)(2,1)}), bf16[1024,3584]{1,0:T(8,128)(2,1)}) %all-gather.6.cloned.1.call-update) | async-done | bytes 7340048 | tf_op jit(solution)/shard_map/all_gather | solution.py:40
  131.8 43.0 %fusion = (f32[1024]{0:T(1024)S(1)}, f32[1024,4752]{0,1:T(8,128)}) fusion(bf16[1024,3584]{1,0:T(8,128)(2,1)} %all-gather.6.cloned.1.call-done, bf16[4752,3584]{1,0:T(8,128)(2,1)} %param.7), kind=kOutput, calls=%fused_computation.8 | convolution fusion | flops 34884698112 | bytes 60870656 | tf_op jit(solution)/shard_map/rd,vd->rv/dot_general | solution.py:38
  174.8 38.4 %pmax.7 = f32[1024]{0:T(1024)S(1)} all-reduce(f32[1024]{0:T(1024)S(1)} %get-tuple-element.9), channel_id=1, replica_groups=mesh['dp'=8,'vocab'=4] {'dp','vocab'}, use_global_device_ids=true, to_apply=%region_3.4 | all-reduce | flops 1024 | bytes 8192 | tf_op jit(solution)/shard_map/pmax | solution.py:46
  213.1 9.5 %exponential_reduce_fusion = (f32[1024]{0:T(1024)S(1)}, f32[1024]{0:T(1024)S(1)}) fusion(f32[1024,4752]{0,1:T(8,128)} %get-tuple-element.10, f32[1024]{0:T(1024)S(1)} %get-tuple-element.9, s32[1024]{0:T(1024)S(1)} %bitcast.14, s32[4752]{0:T(1024)S(1)} %iota_add_fusion), kind=kLoop, calls=%fused_computation | loop fusion | flops 24328192 | bytes 19499584 | tf_op jit(solution)/shard_map/reduce_sum | solution.py:11
  222.7 40.8 %all-reduce = (f32[1024]{0:T(1024)S(1)}, f32[1024]{0:T(1024)S(1)}) all-reduce(f32[1024]{0:T(1024)S(1)} %get-tuple-element.4, f32[1024]{0:T(1024)S(1)} %exponential_multiply_fusion), channel_id=1, replica_groups=mesh['dp'=8,'vocab'=4] {'dp','vocab'}, use_global_device_ids=true, to_apply=%region_1.2 | all-reduce | flops 2048 | bytes 16384 | tf_op jit(solution)/shard_map/psum | solution.py:47
  263.5 0.6 multiply_reduce_fusion
  264.1 0.6 dynamic_slice.6
  264.7 0.6 dynamic_slice.7
  (4 shorter events, 0.0 us)
Async XLA Ops:
  7.2 124.6 %all-gather.6.cloned.1.call-start = ((), (), s32[]{:S(2)}) async-start(), calls=%async_computation | async-start | bytes 8257536 | tf_op jit(solution)/shard_map/all_gather | solution.py:40
Sparse Core Ops, SparseCore 0:
  19.8 111.9 all-gather.5
where the time goes:
time: 275 us; the launch traced here: 274 us
  blocking collectives  166 us (60%)
  matrix products  43 us (16%)
  waiting for transfers between devices  36.2 us (13%)
  between operations  16.5 us (6%)
  other arithmetic  10.8 us (4%)
    dot_general x1, matrix products, body(): jnp.einsum('rd,vd->rv', lax.all_gather(full_rows, 'dp', axis=0, tiled=Tru...  43 us
    psum x1, blocking collectives, body(): lax.psum((total * jnp.exp(peak - top), picked), ('dp', 'vocab'))  40.8 us
    pmax x1, blocking collectives, body(): top = lax.pmax(peak, ('dp', 'vocab'))  38.4 us
    all_gather x1, waiting for transfers between devices, body(): lax.all_gather(full_rows, 'dp', axis=0, tiled=True)  36.2 us
    all_gather x1, blocking collectives, body(): lax.all_gather(response_mask, 'dp', axis=0, tiled=True)  21.4 us
    all_gather x1, blocking collectives, body(): lax.all_gather(rollout_logprobs, 'dp', axis=0, tiled=True)  18.8 us
    all_gather x1, blocking collectives, body(): lax.all_gather(advantages, 'dp', axis=0, tiled=True)  17.3 us
    all_gather x1, blocking collectives, body(): lax.all_gather(token_ids, 'dp', axis=0, tiled=True)  17.1 us
  transfers between devices with their start and end apart: 1, of which 1 were waited for; matrix products, arithmetic and copies ran while one was open for 0% of the time, Pallas kernels for 0%

commit v1 on v0

--- a/solution.py
+++ b/solution.py
@@ -44,7 +44,7 @@
     peak, total, picked = shard_stats(logits, all_ids, own_columns)
     peak, total, picked = (peak, total, picked)
     top = lax.pmax(peak, ("dp", "vocab"))
-    total_sum, picked_sum = lax.psum((total * jnp.exp(peak - top), picked), ("dp", "vocab"))
+    total_sum, picked_sum = lax.psum(lax.psum((total * jnp.exp(peak - top), picked), "dp"), "vocab")
     logprob_all = picked_sum - (top + jnp.log(total_sum))
     own_logp = lax.dynamic_slice_in_dim(logprob_all, own_start, rows_local, 0)
     weight_all, loss_sum, count = token_terms(logprob_all, all_rollout, all_advant, all_mask)

time: 275 us -> 261 us (0.949)
  blocking collectives: 166 us -> 153 us
    psum x1 -> x2, blocking collectives: 40.8 us -> 27.1 us  [the longest x1 21.4 us: body(): lax.psum((total * jnp.exp(peak - top), picked), 'dp')]
where the time goes in v1:
time: 261 us; the launch traced here: 260 us
  blocking collectives  153 us (59%)
  matrix products  43 us (16%)
  waiting for transfers between devices  36.2 us (14%)
  between operations  16.5 us (6%)
  other arithmetic  10.8 us (4%)
    dot_general x1, matrix products, body(): jnp.einsum('rd,vd->rv', lax.all_gather(full_rows, 'dp', axis=0, tiled=Tru...  43 us
    pmax x1, blocking collectives, body(): top = lax.pmax(peak, ('dp', 'vocab'))  38.3 us
    all_gather x1, waiting for transfers between devices, body(): lax.all_gather(full_rows, 'dp', axis=0, tiled=True)  36.2 us
    all_gather x1, blocking collectives, body(): lax.all_gather(response_mask, 'dp', axis=0, tiled=True)  21.4 us
    psum x1, blocking collectives, body(): lax.psum((total * jnp.exp(peak - top), picked), 'dp')  21.4 us
    all_gather x1, blocking collectives, body(): lax.all_gather(rollout_logprobs, 'dp', axis=0, tiled=True)  18.8 us
    all_gather x1, blocking collectives, body(): lax.all_gather(advantages, 'dp', axis=0, tiled=True)  17.3 us
    all_gather x1, blocking collectives, body(): lax.all_gather(token_ids, 'dp', axis=0, tiled=True)  17.1 us
  transfers between devices with their start and end apart: 1, of which 1 were waited for; matrix products, arithmetic and copies ran while one was open for 0% of the time, Pallas kernels for 0%

profile of v1, /device:TPU:0, one launch (start us, length us, event | category | flops | bytes accessed | tf_op | source)
XLA Modules:
  0.0 260.3 jit_solution(3381287871608712470)
XLA Ops:
  7.2 0.0 all-gather.6.cloned.1.call-start
  7.2 12.5 %all_gather.19 = bf16[128,3584]{1,0:T(8,128)(2,1)} all-gather(bf16[128,896]{1,0:T(8,128)(2,1)} %param.6), channel_id=1, replica_groups=mesh['dp'=8,'vocab'=4] {'vocab'}, dimensions={1}, use_global_device_ids=true | all-gather | bytes 1146880 | tf_op jit(solution)/shard_map/all_gather | solution.py:37
  19.7 0.0 all-gather.6.cloned.1.call-update
  19.7 21.4 %all-gather.2 = s32[8,1,128]{2,1,0:T(1,128)S(1)} all-gather(s32[1,1,128]{2,1,0:T(1,128)} %bitcast.15), channel_id=1, replica_groups=mesh['dp'=8,'vocab'=4] {'dp'}, dimensions={0}, use_global_device_ids=true | all-gather | bytes 4608 | tf_op jit(solution)/shard_map/all_gather | solution.py:31
  41.2 0.6 convert_reduce_fusion
  42.4 17.1 %all-gather = s32[8,1,128]{2,1,0:T(1,128)S(1)} all-gather(s32[1,1,128]{2,1,0:T(1,128)} %bitcast.16), channel_id=1, replica_groups=mesh['dp'=8,'vocab'=4] {'dp'}, dimensions={0}, use_global_device_ids=true | all-gather | bytes 4608 | tf_op jit(solution)/shard_map/all_gather | solution.py:30
  59.5 18.8 %all-gather.1 = f32[8,1,128]{2,1,0:T(1,128)S(1)} all-gather(f32[1,1,128]{2,1,0:T(1,128)} %bitcast.17), channel_id=1, replica_groups=mesh['dp'=8,'vocab'=4] {'dp'}, dimensions={0}, use_global_device_ids=true | all-gather | bytes 4608 | tf_op jit(solution)/shard_map/all_gather | solution.py:34
  78.3 17.3 %all-gather.3 = f32[8,1,128]{2,1,0:T(1,128)S(1)} all-gather(f32[1,1,128]{2,1,0:T(1,128)} %bitcast.18), channel_id=1, replica_groups=mesh['dp'=8,'vocab'=4] {'dp'}, dimensions={0}, use_global_device_ids=true | all-gather | bytes 4608 | tf_op jit(solution)/shard_map/all_gather | solution.py:35
  95.6 36.2 %all-gather.6.cloned.1.call-done = bf16[1024,3584]{1,0:T(8,128)(2,1)} async-done(((bf16[128,3584]{1,0:T(8,128)(2,1)}), bf16[1024,3584]{1,0:T(8,128)(2,1)}) %all-gather.6.cloned.1.call-update) | async-done | bytes 7340048 | tf_op jit(solution)/shard_map/all_gather | solution.py:40
  131.8 43.0 %fusion = (f32[1024]{0:T(1024)S(1)}, f32[1024,4752]{0,1:T(8,128)}) fusion(bf16[1024,3584]{1,0:T(8,128)(2,1)} %all-gather.6.cloned.1.call-done, bf16[4752,3584]{1,0:T(8,128)(2,1)} %param.7), kind=kOutput, calls=%fused_computation.8 | convolution fusion | flops 34884698112 | bytes 60870656 | tf_op jit(solution)/shard_map/rd,vd->rv/dot_general | solution.py:38
  174.8 38.3 %pmax.7 = f32[1024]{0:T(1024)S(1)} all-reduce(f32[1024]{0:T(1024)S(1)} %get-tuple-element.11), channel_id=1, replica_groups=mesh['dp'=8,'vocab'=4] {'dp','vocab'}, use_global_device_ids=true, to_apply=%region_4.5 | all-reduce | flops 1024 | bytes 8192 | tf_op jit(solution)/shard_map/pmax | solution.py:46
  213.1 9.5 %exponential_reduce_fusion = (f32[1024]{0:T(1024)S(1)}, f32[1024]{0:T(1024)S(1)}) fusion(f32[1024,4752]{0,1:T(8,128)} %get-tuple-element.12, f32[1024]{0:T(1024)S(1)} %get-tuple-element.11, s32[1024]{0:T(1024)S(1)} %bitcast.14, s32[4752]{0:T(1024)S(1)} %iota_add_fusion), kind=kLoop, calls=%fused_computation | loop fusion | flops 24328192 | bytes 19499584 | tf_op jit(solution)/shard_map/reduce_sum | solution.py:11
  222.7 21.4 %all-reduce = (f32[1024]{0:T(1024)S(1)}, f32[1024]{0:T(1024)S(1)}) all-reduce(f32[1024]{0:T(1024)S(1)} %get-tuple-element.4, f32[1024]{0:T(1024)S(1)} %exponential_multiply_fusion), channel_id=1, replica_groups=mesh['dp'=8,'vocab'=4] {'dp'}, use_global_device_ids=true, to_apply=%region_1.2 | all-reduce | flops 2048 | bytes 16384 | tf_op jit(solution)/shard_map/psum | solution.py:47
  244.0 5.8 %all-reduce.1 = (f32[1024]{0:T(1024)S(1)}, f32[1024]{0:T(1024)S(1)}) all-reduce(f32[1024]{0:T(1024)S(1)} %get-tuple-element.5, f32[1024]{0:T(1024)S(1)} %get-tuple-element.6), channel_id=1, replica_groups=mesh['dp'=8,'vocab'=4] {'vocab'}, use_global_device_ids=true, to_apply=%region_2.3 | all-reduce | flops 2048 | bytes 16384 | tf_op jit(solution)/shard_map/psum | solution.py:47
  249.8 0.6 multiply_reduce_fusion
  250.4 0.6 dynamic_slice.6
  251.0 0.6 dynamic_slice.7
  (4 shorter events, 0.0 us)
Async XLA Ops:
  7.2 124.6 %all-gather.6.cloned.1.call-start = ((), (), s32[]{:S(2)}) async-start(), calls=%async_computation | async-start | bytes 8257536 | tf_op jit(solution)/shard_map/all_gather | solution.py:40
Sparse Core Ops, SparseCore 0:
  19.8 111.9 all-gather.5
